TPU v7x, 32 devices: a whole 2x2x4 slice. The times are simulated.
32 devices in a mesh: rep: 2 (over x), exp: 4 (over z), ten: 4 (over y, core).
Axes of the slice: x: 2, y: 2, z: 4, core: 2. Of those that a mesh axis runs over, the one named last changes fastest.
Arguments:
- hidden_in: bfloat16 [768, 3072], P(('rep', 'exp', 'ten')), parts along dimension 0, may hold values from -6 to 6
- queries: bfloat16 [768, 6144], P(('rep', 'exp', 'ten')), parts along dimension 0, may hold values from -100 to 100
- new_kv: bfloat16 [2, 768, 1024], P(None, ('rep', 'exp', 'ten')), parts along dimension 1, may hold values from -5 to 5
- prefix_kv: bfloat16 [2, 8, 128, 1024], P(None, ('rep', 'exp'), 'ten'), parts along dimension 1, may hold values from -5 to 5
- decode_kv: bfloat16 [2, 128, 48, 1024], P(None, ('rep', 'exp', 'ten')), parts along dimension 1, may hold values from -5 to 5
- prefix_len: int32 [8], P(('rep', 'exp')), parts along dimension 0, may hold values from 2 to 128
- decode_len: int32 [128], P(('rep', 'exp', 'ten')), parts along dimension 0, may hold values from 2 to 48
- out_proj: bfloat16 [6144, 3072], P('ten'), may hold values from -0.078125 to 0.078125
- norm_gain: float32 [3072], replicated, may hold values from 0.5 to 1.5
- router_w: bfloat16 [3072, 8], replicated, may hold values from -0.109375 to 0.109375
- expert_ids: int32 [768, 2], P(('rep', 'exp', 'ten')), parts along dimension 0, may hold values from 0 to 7, all different within a row; in each aligned block of 24 rows (0 to 23, 24 to 47, ...) at most 7 rows name the same one
- w_gate: bfloat16 [8, 3072, 8192], P('exp', None, 'ten'), may hold values from -0.109375 to 0.109375
- w_up: bfloat16 [8, 3072, 8192], P('exp', None, 'ten'), may hold values from -0.109375 to 0.109375
- w_down: bfloat16 [8, 8192, 3072], P('exp', 'ten'), may hold values from -0.0625 to 0.0625
Outputs:
- layer_out: bfloat16 [768, 3072], P(('rep', 'exp', 'ten')), parts along dimension 0
There are 2 independent parts, one for each index of `rep`. A program takes and returns all parts, laid end to end along the dimension named above; an argument that names none is the same for every part. Nothing has to cross between parts.
Inputs may be any that keep to these rules, and one draw needn't show every extreme that they name: `expert_ids`: each row names two different experts. Within each aligned block of 24 rows (the rows of one device) no expert is named by more than 7 rows, and in some block one expert is named by exactly 7 rows.
All inputs are finite; a program needn't handle non-finite values.
Results may differ from a plain program's by a relative error of at most 0.013.
Values may be sent and summed in bfloat16 or wider, within the bound.
No kernel may reach another device: no remote copies, remote signals or barrier semaphores. Data moves between devices by JAX's collectives and lax.ppermute only.
A program may use at most 128 MiB of HBM per device.

v0:
```python
import jax
import jax.numpy as jnp
from jax import lax
from jax.sharding import PartitionSpec as P

HD = 128
CAP = 7
lowest_score = -1e30


def local_softmax(scores, visible):
    masked = jnp.where(visible, scores, lowest_score)
    row_max = jnp.max(masked, axis=-1)
    exponent = jnp.where(visible, jnp.exp(masked - row_max[..., None]), 0.0)
    return (row_max, exponent, jnp.sum(exponent, axis=-1))


def on_device(
    hidden_in,
    queries,
    new_kv,
    prefix_kv,
    decode_kv,
    prefix_len,
    decode_len,
    out_proj,
    norm_gain,
    router_w,
    expert_ids,
    w_gate,
    w_up,
    w_down,
):
    ten_size = lax.axis_size("ten")
    groups = lax.axis_size("exp")
    my_ten = lax.axis_index("ten")
    rows_dev, model_width = hidden_in.shape
    dec_dev = decode_len.shape[0]
    span_dev = rows_dev - dec_dev
    span_rows = span_dev * ten_size
    kv_width = new_kv.shape[2]
    heads_kv = kv_width // HD
    heads_q = queries.shape[1] // HD
    per_kv = heads_q // heads_kv
    score_scale = HD ** (-0.5)
    ctx_len = decode_kv.shape[2]
    own_heads = queries.reshape(rows_dev, heads_kv, per_kv, HD)
    dec_keys = jnp.concatenate([decode_kv[0], new_kv[0, span_dev:, None]], axis=1).reshape(
        dec_dev, ctx_len + 1, heads_kv, HD
    )
    dec_values = jnp.concatenate([decode_kv[1], new_kv[1, span_dev:, None]], axis=1).reshape(
        dec_dev, ctx_len + 1, heads_kv, HD
    )
    dec_scores = (
        jnp.einsum(
            "dcgh,dpch->dcgp", own_heads[span_dev:], dec_keys, preferred_element_type=jnp.float32
        )
        * score_scale
    )
    dec_pos = jnp.arange(ctx_len + 1, dtype=jnp.int32)[None, :]
    dec_visible = ((dec_pos < decode_len[:, None]) | (dec_pos == ctx_len))[:, None, None, :]
    dec_max, dec_exponent, dec_totals = local_softmax(dec_scores, dec_visible)
    dec_partial = jnp.einsum(
        "dcgp,dpch->dcgh",
        dec_exponent.astype(jnp.bfloat16),
        dec_values,
        preferred_element_type=jnp.float32,
    )
    full_prefix, full_fresh = (
        lax.all_gather(prefix_kv[:, 0], "ten", axis=1, tiled=True),
        lax.all_gather(new_kv[:, :span_dev], "ten", axis=1, tiled=True),
    )
    prefix_total = full_prefix.shape[1]
    key_rows = jnp.concatenate([full_prefix[0], full_fresh[0]], axis=0).reshape(
        prefix_total + span_rows, heads_kv, HD
    )
    value_rows = jnp.concatenate([full_prefix[1], full_fresh[1]], axis=0).reshape(
        prefix_total + span_rows, heads_kv, HD
    )
    scores = (
        jnp.einsum(
            "rcgh,pch->rcgp", own_heads[:span_dev], key_rows, preferred_element_type=jnp.float32
        )
        * score_scale
    )
    query_row = my_ten * span_dev + jnp.arange(span_dev, dtype=jnp.int32)[:, None]
    positions = jnp.arange(prefix_total + span_rows, dtype=jnp.int32)[None, :]
    visible = jnp.where(
        positions < prefix_total, positions < prefix_len[0], positions - prefix_total <= query_row
    )[:, None, None, :]
    row_max, exponent, totals = local_softmax(scores, visible)
    span_out = (
        jnp.einsum(
            "rcgp,pch->rcgh",
            exponent.astype(jnp.bfloat16),
            value_rows,
            preferred_element_type=jnp.float32,
        )
        / totals[..., None]
    )
    dec_out = dec_partial / dec_totals[..., None]
    attended_rows = (
        jnp.concatenate([span_out, dec_out], axis=0)
        .reshape(rows_dev, heads_q * HD)
        .astype(jnp.bfloat16)
    )
    attended = lax.all_to_all(attended_rows, "ten", split_axis=1, concat_axis=0, tiled=True)
    row_block = attended
    projected = lax.psum_scatter(
        jnp.dot(row_block, out_proj, preferred_element_type=jnp.float32).astype(jnp.bfloat16),
        "ten",
        scatter_dimension=0,
        tiled=True,
    ).astype(jnp.float32)
    residual = hidden_in.astype(jnp.float32) + projected
    mean_square = jnp.mean(residual * residual, axis=1, keepdims=True)
    normed = (residual * lax.rsqrt(mean_square + 1e-05) * norm_gain).astype(jnp.bfloat16)
    logits = jnp.dot(normed, router_w, preferred_element_type=jnp.float32)
    experts = router_w.shape[1]
    chosen_hot = (expert_ids[:, :, None] == jnp.arange(experts, dtype=jnp.int32)).astype(jnp.int32)
    chosen_logits = jnp.sum(jnp.where(chosen_hot == 1, logits[:, None, :], 0.0), axis=2)
    route_weights = jax.nn.softmax(chosen_logits, axis=1)
    flat_hot = chosen_hot.reshape(rows_dev * 2, experts)
    slot_rank = jnp.sum((jnp.cumsum(flat_hot, axis=0) - flat_hot) * flat_hot, axis=1).reshape(
        rows_dev, 2
    )
    capacity = CAP
    slot_index = jnp.arange(capacity, dtype=jnp.int32)
    assignment = chosen_hot[:, :, :, None] * (slot_rank[:, :, None, None] == slot_index).astype(
        jnp.int32
    )
    placement = jnp.sum(assignment, axis=1)
    local_experts = experts // groups
    placement_split = placement.reshape(rows_dev, groups, local_experts, capacity).astype(
        jnp.bfloat16
    )
    outgoing = jnp.einsum(
        "rnlc,rd->lncd", placement_split, normed, preferred_element_type=jnp.float32
    ).astype(jnp.bfloat16)
    arrived = lax.all_to_all(outgoing, "exp", split_axis=1, concat_axis=1, tiled=True)
    shard_rows = lax.all_gather(arrived, "ten", axis=1, tiled=True)
    gate_act = jnp.einsum("lscd,ldf->lscf", shard_rows, w_gate, preferred_element_type=jnp.float32)
    up_act = jnp.einsum("lscd,ldf->lscf", shard_rows, w_up, preferred_element_type=jnp.float32)
    hidden = (jax.nn.silu(gate_act) * up_act).astype(jnp.bfloat16)
    row_block = hidden
    summed = lax.psum_scatter(
        jnp.einsum("lscf,lfd->slcd", row_block, w_down, preferred_element_type=jnp.float32).astype(
            jnp.bfloat16
        ),
        "ten",
        scatter_dimension=0,
        tiled=True,
    )
    returned = lax.all_to_all(summed, "exp", split_axis=0, concat_axis=0, tiled=True)
    outputs = returned.reshape(experts * capacity, model_width).astype(jnp.float32)
    weight_map = jnp.sum(
        assignment.astype(jnp.float32) * route_weights[:, :, None, None], axis=1
    ).reshape(rows_dev, experts * capacity)
    expert_mix = jnp.dot(
        weight_map, outputs, precision=lax.Precision.HIGHEST, preferred_element_type=jnp.float32
    )
    return (residual + expert_mix).astype(jnp.bfloat16)


def solution(mesh):
    in_specs = (
        P(("rep", "exp", "ten"), None),
        P(("rep", "exp", "ten"), None),
        P(None, ("rep", "exp", "ten"), None),
        P(None, ("rep", "exp"), "ten", None),
        P(None, ("rep", "exp", "ten"), None, None),
        P(("rep", "exp")),
        P(("rep", "exp", "ten")),
        P("ten", None),
        P(),
        P(),
        P(("rep", "exp", "ten"), None),
        P("exp", None, "ten"),
        P("exp", None, "ten"),
        P("exp", "ten", None),
    )
    out_specs = P(("rep", "exp", "ten"), None)
    return jax.shard_map(
        on_device, mesh=mesh, in_specs=in_specs, out_specs=out_specs, check_vma=False
    )
```

profile of v0, /device:TPU:0, one launch (start us, length us, event | category | flops | bytes accessed | tf_op | source)
XLA Modules:
  0.0 201.0 jit_solution(10028590843201728159)
XLA Ops:
  6.6 0.8 fusion.119
  7.3 1.2 fusion.117
  9.0 0.3 copy-done.14
  9.4 0.5 fusion.120
  9.9 0.1 copy.100
  10.1 7.6 %all_gather.10 = bf16[2,80,1024]{2,0,1:T(2,128)(2,1)S(1)} all-gather(bf16[2,20,1024]{2,0,1:T(2,128)(2,1)S(1)} %copy.122), channel_id=1, replica_groups=mesh['rep'=2,'exp'=4,'ten'=4] {'ten'}, dimensions={1}, use_global_device_ids=true | all-gather | bytes 409600 | tf_op jit(solution)/shard_map/all_gather | solution.py:71
  17.7 1.4 slice_reduce_fusion
  19.1 0.1 copy.87
  19.3 7.3 %all-gather = bf16[2,1,128,1024]{3,0,1,2:T(2,128)(2,1)S(1)} all-gather(bf16[2,1,32,1024]{3,0,1,2:T(2,128)(2,1)S(1)} %copy.87), channel_id=2, replica_groups=mesh['rep'=2,'exp'=4,'ten'=4] {'ten'}, dimensions={2}, use_global_device_ids=true | all-gather | bytes 655360 | tf_op jit(solution)/shard_map/all_gather | solution.py:70
  26.6 0.7 fusion.118
  27.3 0.4 copy.121
  27.8 0.2 copy.90
  28.6 0.4 copy.123
  29.1 0.2 copy.93
  29.3 0.3 slice.45
  29.6 0.5 fusion.49
  30.1 0.1 fusion.61
  30.4 0.7 fusion.123
  31.2 0.8 fusion.35
  32.0 0.1 copy.102
  32.1 0.2 convert_element_type.72
  32.3 8.8 %all_to_all.26 = bf16[24,4,1536]{2,0,1:T(8,128)(2,1)S(1)} all-to-all(bf16[24,4,1536]{2,0,1:T(8,128)(2,1)S(1)} %copy.103), channel_id=1, replica_groups=mesh['rep'=2,'exp'=4,'ten'=4] {'ten'}, dimensions={1} | all-to-all | bytes 589824 | tf_op jit(solution)/shard_map/all_to_all | solution.py:107
  41.1 6.2 %convolution_convert_fusion = bf16[96,3072]{1,0:T(8,128)(2,1)} fusion(bf16[96,1536]{1,0:T(8,128)(2,1)S(1)} %bitcast.127, bf16[1536,3072]{1,0:T(8,128)(2,1)} %param.21), kind=kOutput, calls=%fused_computation.10 | convolution fusion | flops 906264576 | bytes 10321920 | tf_op jit(solution)/shard_map/dot_general | solution.py:110
  47.5 0.1 eq.68
  47.8 0.2 select_reduce_fusion
  48.0 0.1 eq.72
  48.2 0.6 copy-done.7
  48.8 0.6 copy-done.9
  49.4 20.6 %reduce-scatter.3.cloned.1.call-done = bf16[24,3072]{1,0:T(8,128)(2,1)} async-done(((bf16[96,3072]{1,0:T(8,128)(2,1)}), bf16[24,3072]{1,0:T(8,128)(2,1)}) %reduce-scatter.3.cloned.1.call-update) | async-done | bytes 147472 | tf_op jit(solution)/shard_map/reduce_scatter | solution.py:109
  70.0 1.1 multiply_reduce_fusion
  71.0 1.0 multiply_convert_fusion
  72.1 0.2 fusion.14
  72.3 0.4 copy.108
  72.7 14.9 %all_to_all.27 = bf16[2,4,7,3072]{3,0,2,1:T(2,128)(2,1)} all-to-all(bf16[2,4,7,3072]{3,0,2,1:T(2,128)(2,1)S(1)} %copy.108), channel_id=1, replica_groups=mesh['rep'=2,'exp'=4,'ten'=4] {'exp'}, dimensions={1} | all-to-all | bytes 688128 | tf_op jit(solution)/shard_map/all_to_all | solution.py:140
  87.7 0.2 all-reduce.3.cloned.1.call-start
  87.9 16.6 %all-gather.3.cloned.1.call-done = bf16[2,16,7,3072]{3,0,2,1:T(2,128)(2,1)} async-done(((bf16[2,4,7,3072]{3,0,2,1:T(2,128)(2,1)}), bf16[2,16,7,3072]{3,0,2,1:T(2,128)(2,1)}) %all-gather.3.cloned.1.call-update) | async-done | bytes 1376272 | tf_op jit(solution)/shard_map/all_gather | solution.py:141
  104.5 10.9 %fusion.6 = f32[2,16,7,2048]{3,1,2,0:T(8,128)S(1)} fusion(bf16[2,3072,2048]{2,1,0:T(8,128)(2,1)} %param.25, bf16[2,16,7,3072]{3,0,2,1:T(2,128)(2,1)} %all-gather.3.cloned.1.call-done), kind=kOutput, calls=%fused_computation.6 | convolution fusion | flops 2818572288 | bytes 28377088 | tf_op jit(solution)/shard_map/lscd,ldf->lscf/dot_general | solution.py:142
  115.4 20.2 %fusion.11 = bf16[16,2,7,3072]{3,0,2,1:T(8,128)(2,1)} fusion(bf16[2,2048,3072]{2,1,0:T(8,128)(2,1)} %param.27, bf16[2,3072,2048]{2,1,0:T(8,128)(2,1)} %param.26, f32[2,16,7,2048]{3,1,2,0:T(8,128)S(1)} %fusion.6, bf16[2,16,7,3072]{3,0,2,1:T(2,128)(2,1)S(1)} %copy-done.1), kind=kOutput, calls=%fused_computation.9 | convolution fusion | flops 5640585216 | bytes 54919168 | tf_op jit(solution)/shard_map/lscf,lfd->slcd/dot_general | solution.py:147
  135.7 0.6 copy-done.15
  136.3 0.6 dynamic-slice
  137.6 0.2 fusion.126
  137.7 38.1 %all-reduce.3.cloned.1.call-done = bf16[16,2,7,3072]{3,0,2,1:T(8,128)(2,1)} async-done(((bf16[16,2,7,3072]{3,0,2,1:T(8,128)(2,1)}), bf16[16,2,7,3072]{3,0,2,1:T(8,128)(2,1)}) %all-reduce.3.cloned.1.call-update) | async-done | bytes 1376272
  175.9 1.3 constant_dynamic-slice_fusion
  177.1 1.0 copy.111
  178.1 4.6 %all-to-all-start.2 = ((bf16[4,2,7,3072]{3,1,2,0:T(2,128)(2,1)}), bf16[4,2,7,3072]{3,1,2,0:T(2,128)(2,1)S(1)}, u32[]{:S(2)}, u32[]{:S(2)}) async-start(bf16[4,2,7,3072]{3,1,2,0:T(2,128)(2,1)} %copy.111), calls=%async_computation.3 | async-start | bytes 688128 | tf_op jit(solution)/shard_map/all_to_all | solution.py:154
  182.9 10.4 %all-to-all-done.2 = bf16[4,2,7,3072]{3,1,2,0:T(2,128)(2,1)S(1)} async-done(((bf16[4,2,7,3072]{3,1,2,0:T(2,128)(2,1)}), bf16[4,2,7,3072]{3,1,2,0:T(2,128)(2,1)S(1)}, u32[]{:S(2)}, u32[]{:S(2)}) %all-to-all-start.2) | async-done | bytes 344096 | tf_op jit(solution)/shard_map/all_to_all | solution.py:154
  193.3 0.1 reshape.204
  193.5 1.0 fusion.15
  (68 shorter events, 1.5 us)
Async XLA Ops:
  6.5 131.0 %copy-start = (bf16[3072,8]{0,1:T(8,128)(2,1)S(1)}, bf16[3072,8]{0,1:T(8,128)(2,1)}, u32[]{:S(2)}) copy-start(bf16[3072,8]{0,1:T(8,128)(2,1)} %param.23) | copy-start | bytes 147460
  6.5 63.4 %reduce-scatter.3.cloned.1.call-start = ((), (), s32[]{:S(2)}) async-start(), calls=%async_computation.4 | async-start | bytes 737280 | tf_op jit(solution)/shard_map/reduce_scatter | solution.py:109
  7.3 1.4 copy-start.4
  8.6 0.7 copy-start.14
  8.9 1.2 copy-start.5
  9.4 9.8 %copy-start.6 = (bf16[2,1,32,1024]{3,2,1,0:T(8,128)(2,1)S(1)}, bf16[2,1,32,1024]{3,2,1,0:T(8,128)(2,1)}, u32[]{:S(2)}) copy-start(bf16[2,1,32,1024]{3,2,1,0:T(8,128)(2,1)} %param.17) | copy-start | bytes 393220
  41.1 6.3 %copy-start.12 = (s32[24,2]{0,1:T(2,128)S(1)}, s32[24,2]{0,1:T(2,128)}, u32[]{:S(2)}) copy-start(s32[24,2]{0,1:T(2,128)} %param.24) | copy-start | bytes 580
  41.1 28.8 %copy-start.2 = (bf16[24,3072]{1,0:T(8,128)(2,1)S(1)}, bf16[24,3072]{1,0:T(8,128)(2,1)}, u32[]{:S(2)}) copy-start(bf16[24,3072]{1,0:T(8,128)(2,1)} %param.14) | copy-start | bytes 442372
  41.1 29.9 %copy-start.11 = (f32[3072]{0:T(1024)S(1)}, f32[3072]{0:T(1024)}, u32[]{:S(2)}) copy-start(f32[3072]{0:T(1024)} %param.22) | copy-start | bytes 36868
  47.4 57.1 %all-gather.3.cloned.1.call-start = ((), (), s32[]{:S(2)}) async-start(), calls=%async_computation.5 | async-start | bytes 1720320 | tf_op jit(solution)/shard_map/all_gather | solution.py:141
  48.2 0.6 copy-start.7
  48.8 0.6 copy-start.9
  87.7 88.2 %all-reduce.3.cloned.1.call-start = ((), (), s32[]{:S(2)}) async-start(), calls=%async_computation.6 | async-start | bytes 2752512
  104.5 10.9 %copy-start.1 = (bf16[2,16,7,3072]{3,0,2,1:T(2,128)(2,1)S(1)}, bf16[2,16,7,3072]{3,0,2,1:T(2,128)(2,1)}, u32[]{:S(2)}) copy-start(bf16[2,16,7,3072]{3,0,2,1:T(2,128)(2,1)} %all-gather.3.cloned.1.call-done) | copy-start | bytes 4128772
  135.6 0.7 copy-start.15
  135.7 47.1 %copy-start.13 = (s32[24,2]{0,1:T(2,128)S(1)}, s32[24,2]{0,1:T(2,128)}, u32[]{:S(2)}) copy-start(s32[24,2]{0,1:T(2,128)} %param.24) | copy-start | bytes 580
  135.7 47.1 %copy-start.8 = (s32[24,2,8]{0,2,1:T(8,128)S(1)}, s32[24,2,8]{0,2,1:T(8,128)}, u32[]{:S(2)}) copy-start(s32[24,2,8]{0,2,1:T(8,128)} %copy-done.7) | copy-start | bytes 4612
  135.7 47.1 %copy-start.10 = (s32[24,2,7]{0,2,1:T(8,128)S(1)}, s32[24,2,7]{0,2,1:T(8,128)}, u32[]{:S(2)}) copy-start(s32[24,2,7]{0,2,1:T(8,128)} %copy-done.9) | copy-start | bytes 4036
  177.1 16.3 %copy-start.3 = (bf16[24,3072]{1,0:T(8,128)(2,1)S(1)}, bf16[24,3072]{1,0:T(8,128)(2,1)}, u32[]{:S(2)}) copy-start(bf16[24,3072]{1,0:T(8,128)(2,1)} %reduce-scatter.3.cloned.1.call-done) | copy-start | bytes 442372
  178.1 15.1 %all-to-all-start.2 = ((bf16[4,2,7,3072]{3,1,2,0:T(2,128)(2,1)}), bf16[4,2,7,3072]{3,1,2,0:T(2,128)(2,1)S(1)}, u32[]{:S(2)}, u32[]{:S(2)}) async-start(bf16[4,2,7,3072]{3,1,2,0:T(2,128)(2,1)} %copy.111), calls=%async_computation.3 | async-start | bytes 688128 | tf_op jit(solution)/shard_map/all_to_all | solution.py:154
Sparse Core Ops, SparseCore 0:
  47.5 22.3 reduce-scatter.2
  87.8 16.6 all-gather.2
  135.8 40.0 all-reduce.2
where the time goes:
time: 201 us
  waiting for transfers between devices  85.7 us (43%)
  matrix products  41.3 us (21%)
  blocking collectives  38.6 us (19%)
  between operations  14.8 us (7%)
  local copies, waits for them, and re-layouts  12.7 us (6%)
  starting transfers between devices  4.87 us (2%)
  other arithmetic  2.9 us (1%)
    unnamed x4, waiting for transfers between devices  38.2 us
    reduce_scatter x1, waiting for transfers between devices, on_device(): lax.psum_scatter(jnp.dot(row_block, out_proj, preferred_element_type=jnp....  20.6 us
    dot_general x1, matrix products, on_device(): jnp.einsum('lscf,lfd->slcd', row_block, w_down, preferred_element_type=jn...  20.2 us
    all_gather x1, waiting for transfers between devices, on_device(): shard_rows = lax.all_gather(arrived, 'ten', axis=1, tiled=True)  16.6 us
    all_to_all x1, blocking collectives, on_device(): lax.all_to_all(outgoing, 'exp', split_axis=1, concat_axis=1, tiled=True)  14.9 us
    dot_general x1, matrix products, on_device(): jnp.einsum('lscd,ldf->lscf', shard_rows, w_gate, preferred_element_type=j...  10.9 us
    all_to_all x1, waiting for transfers between devices, on_device(): lax.all_to_all(summed, 'exp', split_axis=0, concat_axis=0, tiled=True)  10.4 us
    all_to_all x1, blocking collectives, on_device(): lax.all_to_all(attended_rows, 'ten', split_axis=1, concat_axis=0, tiled=T...  8.78 us
  transfers between devices with their start and end apart: 4, of which 4 were waited for; matrix products, arithmetic and copies ran while one was open for 1% of the time, Pallas kernels for 0%

commit v1 on v0

--- a/solution.py
+++ b/solution.py
@@ -138,7 +138,14 @@
         "rnlc,rd->lncd", placement_split, normed, preferred_element_type=jnp.float32
     ).astype(jnp.bfloat16)
     arrived = lax.all_to_all(outgoing, "exp", split_axis=1, concat_axis=1, tiled=True)
-    shard_rows = lax.all_gather(arrived, "ten", axis=1, tiled=True)
+    ways = lax.axis_size("ten")
+    pieces = [arrived]
+    for far in range(1, ways):
+        pieces.append(
+            lax.ppermute(pieces[far - 1], "ten", [(d, (d - 1) % ways) for d in range(ways)])
+        )
+    line = jnp.concatenate(pieces, axis=1)
+    shard_rows = jnp.roll(line, lax.axis_index("ten") * arrived.shape[1], axis=1)
     gate_act = jnp.einsum("lscd,ldf->lscf", shard_rows, w_gate, preferred_element_type=jnp.float32)
     up_act = jnp.einsum("lscd,ldf->lscf", shard_rows, w_up, preferred_element_type=jnp.float32)
     hidden = (jax.nn.silu(gate_act) * up_act).astype(jnp.bfloat16)

time: 201 us -> 214 us (1.065)
  local copies, waits for them, and re-layouts: 12.7 us -> 20.2 us
  starting transfers between devices: 4.87 us -> 8.51 us
    all_gather x1 -> x0, waiting for transfers between devices: 16.6 us -> none  [on_device(): shard_rows = lax.all_gather(arrived, 'ten', axis=1, tiled=True)]
    ppermute x0 -> x3, waiting for transfers between devices: none -> 14.3 us  [on_device(): lax.ppermute(pieces[far - 1], 'ten', [(d, (d - 1) % ways) for d in range(...]
    concatenate x0 -> x1, local copies, waits for them, and re-layouts: none -> 9.26 us  [on_device(): jnp.roll(line, lax.axis_index('ten') * arrived.shape[1], axis=1)]
    ppermute x0 -> x3, starting transfers between devices: none -> 3.87 us  [on_device(): lax.ppermute(pieces[far - 1], 'ten', [(d, (d - 1) % ways) for d in range(...]
    dot_general x1, matrix products: 20.2 us -> 22.7 us  [on_device(): jnp.einsum('lscf,lfd->slcd', row_block, w_down, preferred_element_type=jn...]
    unnamed x41 -> x29, local copies, waits for them, and re-layouts: 5.37 us -> 3.46 us
    unnamed x4 -> x3, waiting for transfers between devices: 38.2 us -> 38.7 us
  transfers between devices with their start and end apart: 4 -> 6, of which waited for: 4 -> 6; matrix products, arithmetic and copies ran while one was open for 1% -> 1% of each run, Pallas kernels for 0% -> 0%
where the time goes in v1:
time: 214 us
  waiting for transfers between devices  85.1 us (40%)
  matrix products  43.4 us (20%)
  blocking collectives  38.5 us (18%)
  local copies, waits for them, and re-layouts  20.2 us (9%)
  between operations  15.1 us (7%)
  starting transfers between devices  8.51 us (4%)
  other arithmetic  2.9 us (1%)
    unnamed x3, waiting for transfers between devices  38.7 us
    dot_general x1, matrix products, on_device(): jnp.einsum('lscf,lfd->slcd', row_block, w_down, preferred_element_type=jn...  22.7 us
    reduce_scatter x1, waiting for transfers between devices, on_device(): lax.psum_scatter(jnp.dot(row_block, out_proj, preferred_element_type=jnp....  21.7 us
    all_to_all x1, blocking collectives, on_device(): lax.all_to_all(outgoing, 'exp', split_axis=1, concat_axis=1, tiled=True)  14.9 us
    ppermute x3, waiting for transfers between devices, on_device(): lax.ppermute(pieces[far - 1], 'ten', [(d, (d - 1) % ways) for d in range(...  14.3 us
    dot_general x1, matrix products, on_device(): jnp.einsum('lscd,ldf->lscf', shard_rows, w_gate, preferred_element_type=j...  10.4 us
    all_to_all x1, waiting for transfers between devices, on_device(): lax.all_to_all(summed, 'exp', split_axis=0, concat_axis=0, tiled=True)  10.4 us
    concatenate x1, local copies, waits for them, and re-layouts, on_device(): jnp.roll(line, lax.axis_index('ten') * arrived.shape[1], axis=1)  9.26 us
  transfers between devices with their start and end apart: 6, of which 6 were waited for; matrix products, arithmetic and copies ran while one was open for 1% of the time, Pallas kernels for 0%

profile of v1, /device:TPU:0, one launch (start us, length us, event | category | flops | bytes accessed | tf_op | source)
XLA Modules:
  0.0 213.8 jit_solution(8026300443002514885)
XLA Ops:
  6.6 0.8 fusion.116
  7.4 1.2 fusion.114
  9.0 0.2 copy-done.8
  9.3 0.5 fusion.117
  9.8 0.1 copy.102
  10.0 7.6 %all_gather.7 = bf16[2,80,1024]{2,0,1:T(2,128)(2,1)S(1)} all-gather(bf16[2,20,1024]{2,0,1:T(2,128)(2,1)S(1)} %copy.125), channel_id=1, replica_groups=mesh['rep'=2,'exp'=4,'ten'=4] {'ten'}, dimensions={1}, use_global_device_ids=true | all-gather | bytes 409600 | tf_op jit(solution)/shard_map/all_gather | solution.py:71
  17.6 1.4 slice_reduce_fusion
  19.1 0.1 copy.89
  19.2 7.3 %all-gather = bf16[2,1,128,1024]{3,0,1,2:T(2,128)(2,1)S(1)} all-gather(bf16[2,1,32,1024]{3,0,1,2:T(2,128)(2,1)S(1)} %copy.89), channel_id=2, replica_groups=mesh['rep'=2,'exp'=4,'ten'=4] {'ten'}, dimensions={2}, use_global_device_ids=true | all-gather | bytes 655360 | tf_op jit(solution)/shard_map/all_gather | solution.py:70
  26.5 0.7 fusion.115
  27.2 0.4 copy.124
  27.7 0.2 copy.92
  28.5 0.4 copy.126
  29.0 0.2 copy.95
  29.2 0.3 slice.45
  29.5 0.5 fusion.43
  30.1 0.1 fusion.55
  30.3 0.7 fusion.120
  31.1 0.8 fusion.22
  32.0 0.2 convert_element_type.72
  32.3 8.8 %all_to_all.26 = bf16[24,4,1536]{2,0,1:T(8,128)(2,1)S(1)} all-to-all(bf16[24,4,1536]{2,0,1:T(8,128)(2,1)S(1)} %copy.105), channel_id=1, replica_groups=mesh['rep'=2,'exp'=4,'ten'=4] {'ten'}, dimensions={1} | all-to-all | bytes 589824 | tf_op jit(solution)/shard_map/all_to_all | solution.py:107
  41.0 6.2 %convolution_convert_fusion = bf16[96,3072]{1,0:T(8,128)(2,1)} fusion(bf16[96,1536]{1,0:T(8,128)(2,1)S(1)} %bitcast.125, bf16[1536,3072]{1,0:T(8,128)(2,1)} %param.21), kind=kOutput, calls=%fused_computation.10 | convolution fusion | flops 906264576 | bytes 10321920 | tf_op jit(solution)/shard_map/dot_general | solution.py:110
  47.7 0.2 select_reduce_fusion
  47.9 0.1 eq.75
  48.1 21.7 %reduce-scatter.3.cloned.1.call-done = bf16[24,3072]{1,0:T(8,128)(2,1)} async-done(((bf16[96,3072]{1,0:T(8,128)(2,1)}), bf16[24,3072]{1,0:T(8,128)(2,1)}) %reduce-scatter.3.cloned.1.call-update) | async-done | bytes 147472 | tf_op jit(solution)/shard_map/reduce_scatter | solution.py:109
  69.8 1.1 multiply_reduce_fusion
  70.9 1.0 multiply_convert_fusion.1
  71.9 0.2 fusion.14
  72.2 0.4 copy.110
  72.6 14.9 %all_to_all.27 = bf16[2,4,7,3072]{3,0,2,1:T(2,128)(2,1)S(1)} all-to-all(bf16[2,4,7,3072]{3,0,2,1:T(2,128)(2,1)S(1)} %copy.110), channel_id=1, replica_groups=mesh['rep'=2,'exp'=4,'ten'=4] {'exp'}, dimensions={1} | all-to-all | bytes 688128 | tf_op jit(solution)/shard_map/all_to_all | solution.py:140
  87.4 0.1 copy.112
  87.6 4.8 %collective-permute-done = bf16[2,4,7,3072]{3,1,2,0:T(4,128)(2,1)S(1)} collective-permute-done((bf16[2,4,7,3072]{3,1,2,0:T(4,128)(2,1)S(1)}, bf16[2,4,7,3072]{3,1,2,0:T(4,128)(2,1)S(1)}, u32[]{:S(2)}, u32[]{:S(2)}) %collective-permute-start) | collective-permute-done | bytes 344096 | tf_op jit(solution)/shard_map/ppermute | solution.py:145
  92.4 1.9 collective-permute-start.1
  94.3 4.8 %collective-permute-done.1 = bf16[2,4,7,3072]{3,1,2,0:T(4,128)(2,1)S(1)} collective-permute-done((bf16[2,4,7,3072]{3,1,2,0:T(4,128)(2,1)S(1)}, bf16[2,4,7,3072]{3,1,2,0:T(4,128)(2,1)S(1)}, u32[]{:S(2)}, u32[]{:S(2)}) %collective-permute-start.1) | collective-permute-done | bytes 344096 | tf_op jit(solution)/shard_map/ppermute | solution.py:145
  99.1 1.9 collective-permute-start.2
  101.0 4.8 %collective-permute-done.2 = bf16[2,4,7,3072]{3,1,2,0:T(4,128)(2,1)S(1)} collective-permute-done((bf16[2,4,7,3072]{3,1,2,0:T(4,128)(2,1)S(1)}, bf16[2,4,7,3072]{3,1,2,0:T(4,128)(2,1)S(1)}, u32[]{:S(2)}, u32[]{:S(2)}) %collective-permute-start.2) | collective-permute-done | bytes 344096 | tf_op jit(solution)/shard_map/ppermute | solution.py:145
  105.8 9.3 %concatenate.55 = bf16[2,32,7,3072]{3,1,2,0:T(8,128)(2,1)} concatenate(bf16[2,4,7,3072]{3,1,2,0:T(4,128)(2,1)S(1)} %copy.112, bf16[2,4,7,3072]{3,1,2,0:T(4,128)(2,1)S(1)} %collective-permute-done, bf16[2,4,7,3072]{3,1,2,0:T(4,128)(2,1)S(1)} %collective-permute-done.1, bf16[2,4,7,3072]{3,1,2,0:T(4,128)(2,1)S(1)} %collective-permute-done.2, bf16[2,4,7,3072]{3,1,2,0:T(4,128)(2,1)S(1)} %copy.112, ...), dimensions={1} | concatenate | bytes 5505024 | tf_op jit(solution)/shard_map/jit(_roll_dynamic)/concatenate | solution.py:148
  115.0 10.4 %fusion.6 = f32[2,16,7,2048]{3,1,2,0:T(8,128)S(1)} fusion(bf16[2,3072,2048]{2,1,0:T(8,128)(2,1)} %param.25, bf16[2,32,7,3072]{3,1,2,0:T(8,128)(2,1)} %concatenate.55, s32[]{:T(128)S(6)} %select_n.50), kind=kOutput, calls=%fused_computation.6 | convolution fusion | flops 2818572288 | bytes 28377092 | tf_op jit(solution)/shard_map/lscd,ldf->lscf/dot_general | solution.py:149
  125.5 22.7 %fusion.11 = bf16[16,2,7,3072]{3,0,2,1:T(8,128)(2,1)} fusion(bf16[2,2048,3072]{2,1,0:T(8,128)(2,1)} %param.27, f32[2,16,7,2048]{3,1,2,0:T(8,128)S(1)} %fusion.6, bf16[2,3072,2048]{2,1,0:T(8,128)(2,1)} %param.26, bf16[2,32,7,3072]{3,1,2,0:T(8,128)(2,1)} %concatenate.55, s32[]{:T(128)S(6)} %select_n.50), kind=kOutput, calls=%fused_computation.9 | convolution fusion | flops 5640585216 | bytes 54919172 | tf_op jit(solution)/shard_map/lscf,lfd->slcd/dot_general | solution.py:154
  148.2 0.6 dynamic-slice
  149.5 0.2 fusion.123
  149.6 38.7 %all-reduce.3.cloned.1.call-done = bf16[16,2,7,3072]{3,0,2,1:T(8,128)(2,1)} async-done(((bf16[16,2,7,3072]{3,0,2,1:T(8,128)(2,1)}), bf16[16,2,7,3072]{3,0,2,1:T(8,128)(2,1)}) %all-reduce.3.cloned.1.call-update) | async-done | bytes 1376272
  188.3 1.3 constant_dynamic-slice_fusion
  189.6 1.0 copy.114
  190.6 4.6 %all-to-all-start.2 = ((bf16[4,2,7,3072]{3,1,2,0:T(2,128)(2,1)}), bf16[4,2,7,3072]{3,1,2,0:T(2,128)(2,1)S(1)}, u32[]{:S(2)}, u32[]{:S(2)}) async-start(bf16[4,2,7,3072]{3,1,2,0:T(2,128)(2,1)} %copy.114), calls=%async_computation.3 | async-start | bytes 688128 | tf_op jit(solution)/shard_map/all_to_all | solution.py:161
  195.3 10.4 %all-to-all-done.2 = bf16[4,2,7,3072]{3,1,2,0:T(2,128)(2,1)S(1)} async-done(((bf16[4,2,7,3072]{3,1,2,0:T(2,128)(2,1)}), bf16[4,2,7,3072]{3,1,2,0:T(2,128)(2,1)S(1)}, u32[]{:S(2)}, u32[]{:S(2)}) %all-to-all-start.2) | async-done | bytes 344096 | tf_op jit(solution)/shard_map/all_to_all | solution.py:161
  205.8 0.1 reshape.204
  205.9 1.0 fusion.15
  (61 shorter events, 1.7 us)
Async XLA Ops:
  6.5 142.9 %copy-start = (bf16[3072,8]{0,1:T(8,128)(2,1)S(1)}, bf16[3072,8]{0,1:T(8,128)(2,1)}, u32[]{:S(2)}) copy-start(bf16[3072,8]{0,1:T(8,128)(2,1)} %param.23) | copy-start | bytes 147460
  6.5 2.2 %copy-start.3 = (bf16[24,6144]{1,0:T(8,128)(2,1)S(1)}, bf16[24,6144]{1,0:T(8,128)(2,1)}, u32[]{:S(2)}) copy-start(bf16[24,6144]{1,0:T(8,128)(2,1)} %param.15) | copy-start | bytes 884740
  6.5 63.3 %reduce-scatter.3.cloned.1.call-start = ((), (), s32[]{:S(2)}) async-start(), calls=%async_computation.4 | async-start | bytes 737280 | tf_op jit(solution)/shard_map/reduce_scatter | solution.py:109
  8.6 0.7 copy-start.8
  8.6 1.3 copy-start.4
  8.9 10.1 %copy-start.5 = (bf16[2,1,32,1024]{3,2,1,0:T(8,128)(2,1)S(1)}, bf16[2,1,32,1024]{3,2,1,0:T(8,128)(2,1)}, u32[]{:S(2)}) copy-start(bf16[2,1,32,1024]{3,2,1,0:T(8,128)(2,1)} %param.17) | copy-start | bytes 393220
  41.0 6.3 %copy-start.7 = (s32[24,2]{0,1:T(2,128)S(1)}, s32[24,2]{0,1:T(2,128)}, u32[]{:S(2)}) copy-start(s32[24,2]{0,1:T(2,128)} %param.24) | copy-start | bytes 580
  41.0 28.8 %copy-start.1 = (bf16[24,3072]{1,0:T(8,128)(2,1)S(1)}, bf16[24,3072]{1,0:T(8,128)(2,1)}, u32[]{:S(2)}) copy-start(bf16[24,3072]{1,0:T(8,128)(2,1)} %param.14) | copy-start | bytes 442372
  41.0 29.9 %copy-start.6 = (f32[3072]{0:T(1024)S(1)}, f32[3072]{0:T(1024)}, u32[]{:S(2)}) copy-start(f32[3072]{0:T(1024)} %param.22) | copy-start | bytes 36868
  47.3 141.0 %all-reduce.3.cloned.1.call-start = ((), (), s32[]{:S(2)}) async-start(), calls=%async_computation.5 | async-start | bytes 2752512
  87.6 4.8 %collective-permute-start = (bf16[2,4,7,3072]{3,1,2,0:T(4,128)(2,1)S(1)}, bf16[2,4,7,3072]{3,1,2,0:T(4,128)(2,1)S(1)}, u32[]{:S(2)}, u32[]{:S(2)}) collective-permute-start(bf16[2,4,7,3072]{3,1,2,0:T(4,128)(2,1)S(1)} %copy.112), channel_id=1, source_target_pairs={{0,3},{1,0},{2,1},{3,2},{4,7},{5,4},{6,5},{7,6},{8,11},{9,8},{10,9... | collective-permute-start | bytes 1032200 | tf_op jit(solution)/shard_map/ppermute | solution.py:145
  92.4 6.7 %collective-permute-start.1 = (bf16[2,4,7,3072]{3,1,2,0:T(4,128)(2,1)S(1)}, bf16[2,4,7,3072]{3,1,2,0:T(4,128)(2,1)S(1)}, u32[]{:S(2)}, u32[]{:S(2)}) collective-permute-start(bf16[2,4,7,3072]{3,1,2,0:T(4,128)(2,1)S(1)} %collective-permute-done), channel_id=1, source_target_pairs={{0,3},{1,0},{2,1},{3,2},{4,7},{5,4},{6,5},{7,6},{8,11},{9,8},{10,9... | collective-permute-start | bytes 1032200 | tf_op jit(solution)/shard_map/ppermute | solution.py:145
  99.1 6.7 %collective-permute-start.2 = (bf16[2,4,7,3072]{3,1,2,0:T(4,128)(2,1)S(1)}, bf16[2,4,7,3072]{3,1,2,0:T(4,128)(2,1)S(1)}, u32[]{:S(2)}, u32[]{:S(2)}) collective-permute-start(bf16[2,4,7,3072]{3,1,2,0:T(4,128)(2,1)S(1)} %collective-permute-done.1), channel_id=1, source_target_pairs={{0,3},{1,0},{2,1},{3,2},{4,7},{5,4},{6,5},{7,6},{8,11},{9,8},{10,9... | collective-permute-start | bytes 1032200 | tf_op jit(solution)/shard_map/ppermute | solution.py:145
  125.5 22.8 %copy-start.9 = (u32[32]{0:T(128)S(1)}, u32[32]{0:T(128)}, u32[]{:S(2)}) copy-start(u32[32]{0:T(128)} %constant.73) | copy-start | bytes 388
  149.6 56.3 %copy-start.2 = (bf16[24,3072]{1,0:T(8,128)(2,1)S(1)}, bf16[24,3072]{1,0:T(8,128)(2,1)}, u32[]{:S(2)}) copy-start(bf16[24,3072]{1,0:T(8,128)(2,1)} %reduce-scatter.3.cloned.1.call-done) | copy-start | bytes 442372
  190.6 15.1 %all-to-all-start.2 = ((bf16[4,2,7,3072]{3,1,2,0:T(2,128)(2,1)}), bf16[4,2,7,3072]{3,1,2,0:T(2,128)(2,1)S(1)}, u32[]{:S(2)}, u32[]{:S(2)}) async-start(bf16[4,2,7,3072]{3,1,2,0:T(2,128)(2,1)} %copy.114), calls=%async_computation.3 | async-start | bytes 688128 | tf_op jit(solution)/shard_map/all_to_all | solution.py:161
Sparse Core Ops, SparseCore 0:
  47.4 22.3 reduce-scatter.2
  148.3 39.9 all-reduce.2
